TPU v7x, 16 devices: a whole 2x2x2 slice. The times are simulated.
16 devices in a mesh: outer: 2 (over z), middle: 2 (over y), inner: 4 (over x, core).
Axes of the slice: x: 2, y: 2, z: 2, core: 2. Of those that a mesh axis runs over, the one named last changes fastest.
Arguments:
- g_embed: float32 [16, 2048, 768], P(('outer', 'middle', 'inner'))
- g_attn: float32 [16, 2, 768, 3072], P(('outer', 'middle', 'inner'))
- g_ffn_in: float32 [16, 2, 768, 3072], P(('outer', 'middle', 'inner'))
- g_ffn_out: float32 [16, 2, 3072, 768], P(('outer', 'middle', 'inner'))
- g_vec: float32 [16, 2, 9984], P(('outer', 'middle', 'inner'))
- m_flat: float32 [15748608], P(('outer', 'middle', 'inner'))
- v_flat: float32 [15748608], P(('outer', 'middle', 'inner'))
- w_flat: float32 [15748608], P(('outer', 'middle', 'inner'))
Outputs:
- output 1: float32 [15748608], P(('outer', 'middle', 'inner'))
- output 2: float32 [15748608], P(('outer', 'middle', 'inner'))
- output 3: float32 [15748608], P(('outer', 'middle', 'inner'))
- output 4: bfloat16 [2048, 768], replicated
- output 5: bfloat16 [2, 768, 3072], replicated
- output 6: bfloat16 [2, 768, 3072], replicated
- output 7: bfloat16 [2, 3072, 768], replicated
- output 8: bfloat16 [2, 9984], replicated
- output 9: bfloat16 [16, 1968576], P(('outer', 'middle', 'inner'))
All inputs are finite; a program needn't handle non-finite values.
Results may differ from a plain program's by a relative error of at most 0.001.
Values are sent between devices in bfloat16 or wider.
A program may use at most 1 GiB of HBM per device.

v0:
```python
import math
import jax
import jax.numpy as jnp
from jax import lax
from jax.sharding import PartitionSpec as P

MESH_AXES = ('outer', 'middle', 'inner')
ADAM_BETA1 = 0.9
ADAM_BETA2 = 0.98
ADAM_EPS = 1e-9
LEARN_RATE = 0.05
ADAM_STEP = 3


def adam_update(grad_mean, m_old, v_old, w_old):
    m_new = ADAM_BETA1 * m_old + (1.0 - ADAM_BETA1) * grad_mean
    v_new = ADAM_BETA2 * v_old + (1.0 - ADAM_BETA2) * (grad_mean * grad_mean)
    m_hat = m_new / (1.0 - ADAM_BETA1 ** ADAM_STEP)
    v_hat = v_new / (1.0 - ADAM_BETA2 ** ADAM_STEP)
    w_new = w_old - LEARN_RATE * m_hat / (jnp.sqrt(v_hat) + ADAM_EPS)
    return m_new, v_new, w_new


def split_tensors(flat_values, shape_list):
    pieces = []
    offset = 0
    for shape in shape_list:
        count = math.prod(shape)
        pieces.append(flat_values[offset:offset + count].reshape(shape))
        offset += count
    return pieces


def own_chip_block(w_tensors, chip_index, num_chips):
    embed_rows = w_tensors[0].shape[0] // num_chips
    block_list = [lax.dynamic_slice_in_dim(w_tensors[0], chip_index * embed_rows, embed_rows, axis=0).reshape(-1)]
    for tensor in w_tensors[1:]:
        block_rows = tensor.shape[1] // num_chips
        block_list.append(lax.dynamic_slice_in_dim(tensor, chip_index * block_rows, block_rows, axis=1).reshape(-1))
    return jnp.concatenate(block_list)[None, :]


def solution(mesh):
    num_devices = mesh.shape['outer'] * mesh.shape['middle'] * mesh.shape['inner']
    num_chips = num_devices // 2

    def local_step(g_embed, g_attn, g_ffn_in, g_ffn_out, g_vec, m_shard, v_shard, w_shard):
        grad_list = (g_embed, g_attn, g_ffn_in, g_ffn_out, g_vec)
        local_flat = jnp.concatenate([gradient.reshape(-1) for gradient in grad_list])
        grad_mean = lax.psum_scatter(local_flat, MESH_AXES, scatter_dimension=0, tiled=True) / num_devices
        m_new, v_new, w_new = adam_update(grad_mean, m_shard, v_shard, w_shard)
        w_full = lax.all_gather(w_new.astype(jnp.bfloat16), MESH_AXES, axis=0, tiled=True)
        w_tensors = split_tensors(w_full, [gradient.shape[1:] for gradient in grad_list])
        device_index = (lax.axis_index('outer') * mesh.shape['middle'] + lax.axis_index('middle')) * mesh.shape['inner'] + lax.axis_index('inner')
        w_chip = own_chip_block(w_tensors, device_index // 2, num_chips)
        return (m_new, v_new, w_new) + tuple(w_tensors) + (w_chip,)

    return jax.shard_map(local_step, mesh=mesh, in_specs=(P(MESH_AXES),) * 8, out_specs=(P(MESH_AXES),) * 3 + (P(),) * 5 + (P(MESH_AXES),), check_vma=False)
```

profile of v0, /device:TPU:0, one launch (start us, length us, event | category | flops | bytes accessed | tf_op | source)
XLA Modules:
  0.0 1147.0 jit_solution(15073375126921214577)
XLA Ops:
  7.2 0.0 all-reduce.7.cloned.1.call-start
  7.2 6.9 reshape.69
  14.1 5.4 constant_dynamic-update-slice_fusion
  19.6 19.5 %copy.17 = f32[192,24,8,128]{3,1,2,0:T(8,128)} copy(f32[192,24,8,128]{3,2,1,0:T(8,128)} %bitcast.14) | data formatting | bytes 37748736
  39.1 0.0 slice-done.10
  39.1 8.0 copy.18
  47.0 19.7 %reshape.72 = f32[4718592]{0:T(1024)} reshape(f32[1,2,3072,768]{3,2,1,0:T(8,128)} %param.11) | data formatting | bytes 37748736 | tf_op jit(solution)/shard_map/reshape | solution.py:49
  66.7 0.1 reshape.73
  66.8 0.0 slice-start
  66.8 0.0 slice-start.1
  66.8 0.0 slice-start.2
  66.9 16.1 %constant_dynamic-update-slice_fusion.5 = f32[15748608]{0:T(1024)} fusion(f32[15748608]{0:T(1024)} %constant_dynamic-update-slice_fusion, f32[4718592]{0:T(1024)} %bitcast.13), kind=kLoop, calls=%fused_computation.8 | loop fusion | bytes 37748736
  83.0 2.5 copy-done
  85.5 9.4 constant_dynamic-update-slice_fusion.4
  94.9 2.1 slice-done.3
  97.0 0.6 slice-done.4
  97.5 6.6 constant_dynamic-update-slice_fusion.3
  104.2 0.6 constant_dynamic-update-slice_fusion.2
  104.8 0.0 all-reduce.7.cloned.1.call-update
  104.8 0.2 all-reduce.5.cloned.1.call-start
  105.1 558.7 %all-reduce.7.cloned.1.call-done = f32[15748608]{0:T(1024)} async-done(((f32[15748608]{0:T(1024)}), f32[15748608]{0:T(1024)}) %all-reduce.7.cloned.1.call-update) | async-done | bytes 62994448
  663.8 9.7 fusion
  673.5 10.2 broadcast.6
  683.7 30.5 %dynamic-update-slice = bf16[15748608]{0:T(1024)(128)(2,1)} dynamic-update-slice(bf16[15748608]{0:T(1024)(128)(2,1)} %broadcast.6, bf16[984288]{0:T(1024)(128)(2,1)S(1)} %get-tuple-element.9, u32[]{:T(128)S(6)} %multiply.8) | dynamic-update-slice | bytes 3937156
  714.2 0.0 all-reduce.5.cloned.1.call-update
  714.3 301.6 %all-reduce.5.cloned.1.call-done = bf16[15748608]{0:T(1024)(128)(2,1)} async-done(((bf16[15748608]{0:T(1024)(128)(2,1)}), bf16[15748608]{0:T(1024)(128)(2,1)}) %all-reduce.5.cloned.1.call-update) | async-done | bytes 31497232
  1015.9 1.9 slice-done.5
  1017.7 3.8 slice.26
  1021.5 20.0 %fusion.1 = (bf16[4718592]{0:T(1024)(128)(2,1)}, bf16[4718592]{0:T(1024)(128)(2,1)}, bf16[4718592]{0:T(1024)(128)(2,1)}) fusion(bf16[15748608]{0:T(1024)(128)(2,1)} %all-reduce.5.cloned.1.call-done), kind=kLoop, calls=%fused_computation.19 | loop fusion | bytes 56623104 | tf_op jit(solution)/shard_map/slice | solution.py:29
  1041.6 14.8 %reshape.74 = bf16[2,768,3072]{2,1,0:T(8,128)(2,1)} reshape(bf16[4718592]{0:T(1024)(128)(2,1)} %get-tuple-element.15) | data formatting | bytes 18874368 | tf_op jit(solution)/shard_map/reshape | solution.py:29
  1056.3 14.8 %reshape.75 = bf16[2,768,3072]{2,1,0:T(8,128)(2,1)} reshape(bf16[4718592]{0:T(1024)(128)(2,1)} %get-tuple-element.14) | data formatting | bytes 18874368 | tf_op jit(solution)/shard_map/reshape | solution.py:29
  1071.1 16.8 %reshape.76 = bf16[2,3072,768]{2,1,0:T(8,128)(2,1)} reshape(bf16[4718592]{0:T(1024)(128)(2,1)} %get-tuple-element.13) | data formatting | bytes 18874368 | tf_op jit(solution)/shard_map/reshape | solution.py:29
  1087.9 0.7 reshape.77
  1088.6 1.0 constant_dynamic-slice_fusion.4
  1089.6 0.3 reshape.78
  1089.9 0.8 constant_dynamic-update-slice_fusion.1
  1090.7 1.8 constant_dynamic-slice_fusion.2
  1092.5 0.2 copy.19
  1092.7 0.2 copy.20
  1092.9 1.4 constant_dynamic-slice_fusion.1
  1094.3 2.0 reshape.81
  1096.3 0.9 constant_dynamic-slice_fusion
  1097.2 0.1 reshape.82
  1097.3 1.2 constant_dynamic-update-slice_fusion.9
  1098.4 1.1 constant_dynamic-update-slice_fusion.8
  1099.6 1.1 constant_dynamic-update-slice_fusion.7
  1100.7 0.6 constant_dynamic-update-slice_fusion.6
  1101.3 38.9 %broadcast_in_dim.3 = bf16[1,1968576]{1,0:T(2,128)(2,1)} reshape(bf16[1968576]{0:T(1024)(128)(2,1)} %constant_dynamic-update-slice_fusion.6) | data formatting | bytes 7874304 | tf_op jit(solution)/shard_map/broadcast_in_dim | solution.py:40
  (24 shorter events, 0.0 us)
Async XLA Ops:
  7.2 656.6 %all-reduce.7.cloned.1.call-start = ((), (), s32[]{:S(2)}) async-start(), calls=%async_computation.1 | async-start | bytes 125992960
  14.1 24.9 %slice-start.7 = ((s8[18874368]{0:T(1024)(128)(4,1)}), s8[4194304]{0:T(1024)(128)(4,1)S(1)}, s32[]{:S(2)}) async-start(s8[18874368]{0:T(1024)(128)(4,1)} %bitcast.15), calls=%async_computation.9 | async-start | bytes 8388608
  14.1 24.9 %slice-start.8 = ((s8[18874368]{0:T(1024)(128)(4,1)}), s8[4194304]{0:T(1024)(128)(4,1)S(1)}, s32[]{:S(2)}) async-start(s8[18874368]{0:T(1024)(128)(4,1)} %bitcast.15), calls=%async_computation.10 | async-start | bytes 8388608
  19.5 19.5 %slice-start.9 = ((s8[18874368]{0:T(1024)(128)(4,1)}), s8[4194304]{0:T(1024)(128)(4,1)S(1)}, s32[]{:S(2)}) async-start(s8[18874368]{0:T(1024)(128)(4,1)} %bitcast.15), calls=%async_computation.11 | async-start | bytes 8388608
  19.5 19.5 %slice-start.10 = ((s8[18874368]{0:T(1024)(128)(4,1)}), s8[4194304]{0:T(1024)(128)(4,1)S(1)}, s32[]{:S(2)}) async-start(s8[18874368]{0:T(1024)(128)(4,1)} %bitcast.15), calls=%async_computation.12 | async-start | bytes 8388608
  19.5 19.5 %slice-start.11 = ((s8[18874368]{0:T(1024)(128)(4,1)}), s8[2097152]{0:T(1024)(128)(4,1)S(1)}, s32[]{:S(2)}) async-start(s8[18874368]{0:T(1024)(128)(4,1)} %bitcast.15), calls=%async_computation.13 | async-start | bytes 4194304
  47.0 19.7 %copy-start.2 = (f32[1,2,9984]{2,1,0:T(2,128)S(1)}, f32[1,2,9984]{2,1,0:T(2,128)}, u32[]{:S(2)}) copy-start(f32[1,2,9984]{2,1,0:T(2,128)} %param.12) | copy-start | bytes 239620
  66.8 18.7 %copy-start = (f32[192,24,8,128]{3,1,2,0:T(8,128)S(1)}, f32[192,24,8,128]{3,1,2,0:T(8,128)}, u32[]{:S(2)}) copy-start(f32[192,24,8,128]{3,1,2,0:T(8,128)} %copy.18) | copy-start | bytes 56623108
  66.8 28.0 %slice-start = ((s8[18874368]{0:T(1024)(128)(4,1)}), s8[4194304]{0:T(1024)(128)(4,1)S(1)}, s32[]{:S(2)}) async-start(s8[18874368]{0:T(1024)(128)(4,1)} %bitcast.10), calls=%async_computation.2 | async-start | bytes 8388608
  66.8 28.0 %slice-start.1 = ((s8[18874368]{0:T(1024)(128)(4,1)}), s8[4194304]{0:T(1024)(128)(4,1)S(1)}, s32[]{:S(2)}) async-start(s8[18874368]{0:T(1024)(128)(4,1)} %bitcast.10), calls=%async_computation.3 | async-start | bytes 8388608
  66.8 28.0 %slice-start.2 = ((s8[18874368]{0:T(1024)(128)(4,1)}), s8[4194304]{0:T(1024)(128)(4,1)S(1)}, s32[]{:S(2)}) async-start(s8[18874368]{0:T(1024)(128)(4,1)} %bitcast.10), calls=%async_computation.4 | async-start | bytes 8388608
  85.5 11.5 %slice-start.3 = ((s8[18874368]{0:T(1024)(128)(4,1)}), s8[4194304]{0:T(1024)(128)(4,1)S(1)}, s32[]{:S(2)}) async-start(s8[18874368]{0:T(1024)(128)(4,1)} %bitcast.10), calls=%async_computation.5 | async-start | bytes 8388608
  85.5 12.1 %slice-start.4 = ((s8[18874368]{0:T(1024)(128)(4,1)}), s8[2097152]{0:T(1024)(128)(4,1)S(1)}, s32[]{:S(2)}) async-start(s8[18874368]{0:T(1024)(128)(4,1)} %bitcast.10), calls=%async_computation.6 | async-start | bytes 4194304
  104.8 911.0 %all-reduce.5.cloned.1.call-start = ((), (), s32[]{:S(2)}) async-start(), calls=%async_computation | async-start | bytes 62996480
  1015.9 1.9 slice-start.5
  1071.1 16.8 %slice-start.6 = ((bf16[15748608]{0:T(1024)(128)(2,1)}), bf16[19968]{0:T(1024)(128)(2,1)S(1)}, s32[]{:S(2)}) async-start(bf16[15748608]{0:T(1024)(128)(2,1)} %all-reduce.5.cloned.1.call-done), calls=%async_computation.8 | async-start | bytes 81920 | tf_op jit(solution)/shard_map/slice | solution.py:29
  1096.3 3.2 copy-start.1
Sparse Core Ops, SparseCore 0:
  104.9 558.7 all-reduce.6
  714.3 301.4 all-reduce.4
where the time goes:
time: 1150 us
  waiting for transfers between devices  860 us (75%)
  local copies, waits for them, and re-layouts  262 us (23%)
  between operations  14.2 us (1%)
    unnamed x4, waiting for transfers between devices  860 us
    unnamed x40, local copies, waits for them, and re-layouts  116 us
    reshape x4, local copies, waits for them, and re-layouts, split_tensors(): pieces.append(flat_values[offset:offset + count].reshape(shape))  47 us
    broadcast_in_dim x1, local copies, waits for them, and re-layouts, own_chip_block(): return jnp.concatenate(block_list)[None, :]  38.9 us
    reshape x3, local copies, waits for them, and re-layouts, local_step(): gradient.reshape(-1)  26.6 us
    slice x6, local copies, waits for them, and re-layouts, split_tensors(): pieces.append(flat_values[offset:offset + count].reshape(shape))  25.7 us
  transfers between devices with their start and end apart: 2, of which 2 were waited for; matrix products, arithmetic and copies ran while one was open for 0% of the time, Pallas kernels for 0%

commit v1 on v0

v1 whole, which is shorter than its diff:
```python
import jax
import jax.numpy as jnp
from jax import lax
from jax.experimental import pallas as pl
from jax.experimental.pallas import tpu as pltpu
from jax.sharding import PartitionSpec as P

MESH_AXES = ('outer', 'middle', 'inner')
ADAM_BETA1 = 0.9
ADAM_BETA2 = 0.98
ADAM_EPS = 1e-9
LEARN_RATE = 0.05
ADAM_STEP = 3

TILE = (8, 128)
LANES = TILE[1]
TILE_SIZE = 1024
ROUNDS = 10
TILES = 96
SLOTS = ((0, 48, 0, 0), (1, 24, 48, 384), (2, 24, 72, 576))
BLOCKS = 8 * TILES
TENSOR_GROUPS = (0, 16, 64, 112, 160)
ROWS = 768
FLAT = ROUNDS * ROWS * 128
SHARD = 984288
STEP = SHARD - FLAT
BTAIL = 16 * STEP
BROWS = 160
BPAD = BROWS - BTAIL // 128
RAW_ROWS = ROWS + BROWS
OUT_ROWS = ROUNDS * ROWS + 2 * BROWS
NACC = 5
STAGES = ROUNDS + 6
MESH = pl.DeviceIdType.MESH


def loop(count, body, **options):
    lax.fori_loop(0, count, lambda i, carry: (body(i), carry)[1], None, **options)


def top(n):
    return pl.ds(0, n)


def device_number():
    return (lax.axis_index('outer') * 2 + lax.axis_index('middle')) * 4 + lax.axis_index('inner')


def mesh_id(d):
    return (d // 8, (d // 4) % 2, d % 4)


def adam_update(grad_mean, m_old, v_old, w_old):
    m_new = ADAM_BETA1 * m_old + (1.0 - ADAM_BETA1) * grad_mean
    v_new = ADAM_BETA2 * v_old + (1.0 - ADAM_BETA2) * (grad_mean * grad_mean)
    m_hat = m_new / (1.0 - ADAM_BETA1 ** ADAM_STEP)
    v_hat = v_new / (1.0 - ADAM_BETA2 ** ADAM_STEP)
    w_new = w_old - LEARN_RATE * m_hat / (jnp.sqrt(v_hat) + ADAM_EPS)
    return m_new, v_new, w_new


def axis_weights(a):
    return ((a - 1) * (a - 2)) // 2, a * (2 - a), (a * (a - 1)) // 2


def pick(values, a):
    e0, e1, e2 = axis_weights(a)
    return values[0] * e0 + values[1] * e1 + values[2] * e2


def chip_bits(d):
    return (d // 2) % 2, (d // 4) % 2, d // 8


def comm_kernel(ge, ga, gf, gh, gb, m1, v1, w1, mvwb,
                wst, m_out, v_out, w_out, wb_out,
                acc, sib, l1, l2, l3, flat_in, raw, mv, flat_out, heads, wt, bs, bl, bout, wbs, wbl,
                own_sem, sib_send, sib_recv, rs_send, rs_recv, ag_send, ag_recv, fw_send, fw_recv,
                loc_sem, in_sem, out_sem, b_send, b_recv, end_sem, head_sem, free_sem):
    me = device_number()
    core = me % 2
    mate = me + 1 - 2 * core
    bits = chip_bits(me)
    deltas = tuple(m * (1 - 2 * b) for m, b in zip((2, 4, 8), bits))
    partners = (mate,) + tuple(me + d for d in deltas)
    grads = (ge, ga, gf, gh)
    olds = tuple(enumerate((m1, v1, w1)))
    outs = tuple(enumerate((m_out, v_out, w_out)))
    shift_rows = (STEP * me) // LANES
    shift_lanes = (STEP * me) % LANES
    back_lanes = (LANES - shift_lanes) % LANES
    lane = lax.broadcasted_iota(jnp.int32, TILE, 1)

    barrier = pltpu.get_barrier_semaphore()
    for other in partners + ((me + 1) % 16, (me + 15) % 16):
        pl.semaphore_signal(barrier, inc=1, device_id=mesh_id(other), device_id_type=MESH)
    pl.semaphore_wait(barrier, 6)

    def remote(src, dst, ssem, rsem, dev):
        return pltpu.make_async_remote_copy(src_ref=src, dst_ref=dst, send_sem=ssem, recv_sem=rsem,
                                            device_id=mesh_id(dev), device_id_type=MESH)

    def turned(r):
        steps = [pick(deltas, lax.rem(r + j, 3)) for j in range(3)]
        return [[steps[(t + j) % 3] for j in range(3)] for t in range(3)]

    def any_tiles(n):
        return ga.at[top(n)]

    def rs_wait(r, j):
        half = acc.at[0, top(BLOCKS // 2 >> j)]
        remote(half, half, rs_send.at[r, j], rs_recv.at[r, 0, j], mate).wait_send()

    def load_round(r):
        a = r % NACC
        b = r % 2

        steps = turned(r)

        def body(back):
            rel = 7 - back
            betas = (rel // 4, (rel // 2) % 2, rel % 2)
            for t, n, first, base in SLOTS:
                d = me + sum(beta * step for beta, step in zip(betas, steps[t]))
                at = pl.ds(base + rel * n, n)
                for other in (False, True):
                    group = ROUNDS * (d + (mate - me if other else 0)) + r
                    for ref, lo, hi in zip(grads, TENSOR_GROUPS, TENSOR_GROUPS[1:]):
                        @pl.when((group >= lo) & (group < hi))
                        def _(ref=ref, lo=lo, other=other, group=group):
                            src = ref.at[pl.ds((group - lo) * TILES + first, n)]
                            if other:
                                remote(src, sib.at[b, at], sib_send.at[b], sib_recv.at[b, rel // 4], mate).start()
                            else:
                                pltpu.make_async_copy(src, acc.at[a, at], own_sem.at[a, rel // 4]).start()

        loop(8, body)

    def add_range(dst, src, n):
        def body(i):
            at = pl.ds(i * 8, 8)
            dst[at] = dst[at] + src[at]

        loop(n // 8, body)

    def when_round(r):
        return pl.when((r >= 0) & (r < ROUNDS))

    def old_copy(ref, r, i, skip):
        n = (RAW_ROWS - skip) * LANES
        at = ((r % 2 * 3 + i) * RAW_ROWS + skip) * LANES
        return pltpu.make_async_copy(ref.at[pl.ds((r * ROWS - BROWS + skip) * LANES, n)], flat_in.at[pl.ds(at, n)],
                                     in_sem.at[r % 2])

    def old_rows(r, skip):
        for i, ref in olds:
            old_copy(ref, r, i, skip).wait()

        def body(k):
            row = skip + k * 8
            for i, ref in olds:
                at = ((r % 2 * 3 + i) * RAW_ROWS + row) * LANES
                raw[i, pl.ds(row, 8), :] = flat_in[pl.ds(pl.multiple_of(at, TILE_SIZE), TILE_SIZE)].reshape(TILE)

        loop((RAW_ROWS - skip) // 8, body)

    def out_copy(ref, b, i, r, n):
        at = pl.multiple_of((r * ROWS + BROWS - 1 - shift_rows) * LANES, LANES)
        return pltpu.make_async_copy(flat_out.at[pl.ds((b * 3 + i) * ROWS * LANES, n * LANES)], ref.at[pl.ds(at, n * LANES)],
                                     out_sem.at[b])

    def put_out(b, r, n):
        def body(k):
            for i, ref in outs:
                low = pltpu.roll(mv[i, pl.ds(k * 8 + 7, 8), :], back_lanes, 1)
                high = pltpu.roll(mv[i, pl.ds(k * 8 + 8, 8), :], back_lanes, 1)
                at = ((b * 3 + i) * ROWS + k * 8) * LANES
                both = jnp.where(lane < LANES - shift_lanes, low, high)
                flat_out[pl.ds(pl.multiple_of(at, TILE_SIZE), TILE_SIZE)] = both.reshape(TILE_SIZE)

        loop(n // 8, body)
        for i, ref in outs:
            out_copy(ref, b, i, r, n).start()

    def wait_out(b, n):
        for i, ref in outs:
            out_copy(ref, b, i, 0, n).wait()

    load_round(0)

    @pl.when(me < 15)
    def _():
        remote(mvwb, raw.at[:, top(BROWS)], end_sem.at[0], end_sem.at[1], me + 1).start()

    def stage(s):
        nxt = s + 1

        @pl.when((nxt >= NACC) & (nxt < ROUNDS))
        def _():
            for j in range(3):
                rs_wait(nxt - NACC, j)

        @pl.when((nxt >= 2) & (nxt < ROUNDS))
        def _():
            remote(any_tiles(BLOCKS), sib.at[0], sib_send.at[nxt % 2], sib_recv.at[0, 0], mate).wait_send()
            pl.semaphore_wait(free_sem, 1)

        @pl.when(nxt < ROUNDS)
        def _():
            load_round(nxt)

        @pl.when(s == 2)
        def _():
            for i, ref in olds:
                old_copy(ref, 0, i, BROWS).start()

        @pl.when((s > 2) & (s < ROUNDS + 2))
        def _():
            for i, ref in olds:
                old_copy(ref, s - 2, i, 0).start()

        @when_round(s)
        def _():
            r, a, b = s, s % NACC, s % 2
            steps = turned(r)

            def loaded(part):
                src, half = any_tiles(BLOCKS // 2), top(BLOCKS // 2)
                pltpu.make_async_copy(src, acc.at[a, half], own_sem.at[a, part]).wait()
                remote(src, sib.at[b, half], sib_send.at[b], sib_recv.at[b, part], mate).wait_recv()

            loaded(1)
            for t, n, first, base in SLOTS:
                hi = pl.ds(base + 4 * n, 4 * n)
                add_range(acc.at[a, hi], sib.at[b, hi], 4 * n)
            for t, n, first, base in SLOTS:
                remote(acc.at[a, pl.ds(base + 4 * n, 4 * n)], l1.at[r, pl.ds(base // 2, 4 * n)],
                       rs_send.at[r, 0], rs_recv.at[r, t, 0], me + steps[t][0]).start()
            loaded(0)
            for t, n, first, base in SLOTS:
                lo = pl.ds(base, 4 * n)
                add_range(acc.at[a, lo], sib.at[b, lo], 4 * n)

            @pl.when(r + 2 < ROUNDS)
            def _():
                pl.semaphore_signal(free_sem, inc=1, device_id=mesh_id(mate), device_id_type=MESH)

        for j, land, out in ((1, l1, l2), (2, l2, l3)):
            @when_round(s - j)
            def _(j=j, land=land, out=out):
                r = s - j
                a = r % NACC
                keep = 4 >> j
                steps = turned(r)
                for t, n, first, base in SLOTS:
                    here = land.at[r, pl.ds(base >> j, 2 * keep * n)]
                    remote(here, here, rs_send.at[r, j - 1], rs_recv.at[r, t, j - 1], mate).wait_recv()
                    add_range(acc.at[a, pl.ds(base + keep * n, keep * n)],
                              land.at[r, pl.ds((base >> j) + keep * n, keep * n)], keep * n)
                for t, n, first, base in SLOTS:
                    remote(acc.at[a, pl.ds(base + keep * n, keep * n)], out.at[r, pl.ds(base >> (j + 1), keep * n)],
                           rs_send.at[r, j], rs_recv.at[r, t, j], me + steps[t][j]).start()
                for t, n, first, base in SLOTS:
                    add_range(acc.at[a, pl.ds(base, keep * n)], land.at[r, pl.ds(base >> j, keep * n)], keep * n)

        @when_round(s - 3)
        def _():
            r = s - 3
            a, b = r % NACC, r % 2

            @pl.when(r == 0)
            def _():
                old_rows(0, BROWS)

            @pl.when((r == 0) & (me > 0))
            def _():
                remote(mvwb, raw.at[:, top(BROWS)], end_sem.at[0], end_sem.at[1], mate).wait_recv()

            @pl.when(r > 0)
            def _():
                old_rows(r, 0)

            @pl.when((r == 1) & (me > 0))
            def _():
                remote(mv.at[:, pl.ds(8, BROWS)], heads, head_sem.at[0], head_sem.at[1], mate).wait_send()

            for i, ref in outs:
                mv[i, pl.ds(7, 1), :] = mv[i, pl.ds(ROWS + 7, 1), :]
            for t, n, first, base in SLOTS:
                here = l3.at[r, pl.ds(first, n)]
                remote(here, here, rs_send.at[r, 2], rs_recv.at[r, t, 2], mate).wait_recv()
            steps = turned(r)
            group = ROUNDS * me + r
            wide = (group >= TENSOR_GROUPS[1]) & (group < TENSOR_GROUPS[3])

            def adam_pass(stride):
                for t, n, first, base in SLOTS:
                    def body(u, first=first, base=base):
                        unit = first // 6 + u
                        if stride == 6:
                            row = unit * 48
                        else:
                            row = (unit // 4) * 192 + (unit % 4) * 6
                        for j in range(6):
                            old = []
                            for i, ref in olds:
                                at = row + j + BROWS - shift_rows
                                here = pltpu.roll(raw[i, pl.ds(at, 8, stride=stride), :], shift_lanes, 1)
                                prev = pltpu.roll(raw[i, pl.ds(at - 1, 8, stride=stride), :], shift_lanes, 1)
                                old.append(jnp.where(lane >= shift_lanes, here, prev))
                            tile = acc[a, base + u * 6 + j] + l3[r, unit * 6 + j]
                            new = adam_update(tile * (1.0 / 16.0), *old)
                            for i, ref in olds:
                                mv[i, pl.ds(row + j + 8, 8, stride=stride), :] = new[i]
                            wt[r, unit * 6 + j] = new[2].astype(jnp.bfloat16)

                    loop(n // 6, body)

            @pl.when(wide)
            def _():
                adam_pass(24)

            @pl.when(jnp.logical_not(wide))
            def _():
                adam_pass(6)

            for t, n, first, base in SLOTS:
                src = wt.at[r, pl.ds(first, n)]
                remote(src, wst.at[core, r, pl.ds(base + n, n)], ag_send.at[r, 0], ag_recv.at[r, t, 0],
                       me + steps[t][0]).start()
                remote(src, wst.at[core, r, pl.ds(base, n)], fw_send.at[r, 0], fw_recv.at[r, 0], mate).start()
                pltpu.make_async_copy(src, wst.at[core, r, pl.ds(base, n)], loc_sem.at[r]).start()

            @pl.when((r == 0) & (me > 0))
            def _():
                remote(mv.at[:, pl.ds(8, BROWS)], heads, head_sem.at[0], head_sem.at[1], me - 1).start()

            @pl.when(r >= 2)
            def _():
                wait_out(b, ROWS)

            put_out(b, r, ROWS)

        @pl.when((s == ROUNDS + 3) & (me < 15))
        def _():
            remote(mvwb, raw.at[:, top(BROWS)], end_sem.at[0], end_sem.at[1], mate).wait_send()
            remote(mv.at[:, pl.ds(8, BROWS)], heads, head_sem.at[0], head_sem.at[1], mate).wait_recv()

        @pl.when(s == ROUNDS + 3)
        def _():
            wait_out(0, ROWS)
            for i, ref in outs:
                mv[i, pl.ds(7, 1), :] = mv[i, pl.ds(ROWS + 7, 1), :]
                mv[i, pl.ds(8, BROWS), :] = heads[i]
            put_out(0, ROUNDS, BROWS)

        for j in (1, 2, 3):
            @when_round(s - 3 - j)
            def _(j=j):
                r = s - 3 - j
                got = 1 << (j - 1)
                steps = turned(r)
                if j == 1:
                    pltpu.make_async_copy(wt.at[r], wst.at[core, r, top(TILES)], loc_sem.at[r]).wait()
                for t, n, first, base in SLOTS:
                    here = wst.at[core, r, pl.ds(base + got * n, got * n)]
                    remote(here, here, ag_send.at[r, j - 1], ag_recv.at[r, t, j - 1], mate).wait_recv()
                    if j < 3:
                        remote(wst.at[core, r, pl.ds(base, 2 * got * n)],
                               wst.at[core, r, pl.ds(base + 2 * got * n, 2 * got * n)],
                               ag_send.at[r, j], ag_recv.at[r, t, j], me + steps[t][j]).start()
                    remote(here, here, fw_send.at[r, j], fw_recv.at[r, j], mate).start()

        for j in range(9):
            @pl.when(s == j)
            def _(j=j):
                if j > 0:
                    i = j - 1
                    land = bl.at[i] if i < 4 else wbl.at[i - 4]
                    remote(land, land, b_send.at[i], b_recv.at[i], mate).wait_recv()
                if j < 4:
                    src = gb
                    if j > 0:
                        src = bs.at[j - 1]
                        src[...] = (gb[...] if j == 1 else bs[j - 2]) + bl[j - 1]
                    remote(src, bl.at[j], b_send.at[j], b_recv.at[j], partners[j]).start()
                elif j < 8:
                    if j == 4:
                        new = adam_update((bs[2] + bl[3]) * (1.0 / 16.0), mvwb[0], mvwb[1], mvwb[2])
                        for i, ref in outs:
                            bout[i] = new[i]
                        keep = jnp.broadcast_to(me, (BROWS, LANES)) == 15
                        wbs[0] = jnp.where(keep, new[2], 0.0).astype(jnp.bfloat16)

                        @pl.when(me == 15)
                        def _():
                            for i, ref in outs:
                                heads[i, top(BROWS - BPAD), :] = bout[i, pl.ds(BPAD, BROWS - BPAD), :]
                    else:
                        wbs[j - 4] = wbs[j - 5] + wbl[j - 5]
                    remote(wbs.at[j - 4], wbl.at[j - 4], b_send.at[j], b_recv.at[j], partners[j - 4]).start()
                else:
                    wb_out[...] = wbs[3] + wbl[3]

    loop(STAGES, stage)

    for j in range(4):
        remote(gb, bl.at[j], b_send.at[j], b_recv.at[j], mate).wait_send()
        remote(wbs.at[j], wbl.at[j], b_send.at[4 + j], b_recv.at[4 + j], mate).wait_send()
    for b in range(2):
        remote(any_tiles(BLOCKS), sib.at[0], sib_send.at[b], sib_recv.at[0, 0], mate).wait_send()

    def drain(r):
        @pl.when(r >= ROUNDS - NACC)
        def _():
            for j in range(3):
                rs_wait(r, j)

        for j in range(3):
            part = wst.at[0, 0, top(TILES << j)]
            remote(part, part, ag_send.at[r, j], ag_recv.at[r, 0, j], mate).wait_send()
        for j in range(4):
            part = wst.at[0, 0, top(TILES << max(j - 1, 0))]
            remote(part, part, fw_send.at[r, j], fw_recv.at[r, j], mate).wait_send()
            remote(part, part, fw_send.at[r, j], fw_recv.at[r, j], mate).wait_recv()

    loop(ROUNDS, drain)
    wait_out(1, ROWS)
    wait_out(0, BROWS)


def comm_call(grads, gb, olds, mvwb):
    any_spec = pl.BlockSpec(memory_space=pl.ANY)
    vmem_spec = pl.BlockSpec(memory_space=pltpu.VMEM)
    f32, bf16 = jnp.float32, jnp.bfloat16
    dma = pltpu.SemaphoreType.DMA
    flat = jax.ShapeDtypeStruct((OUT_ROWS * LANES,), f32)
    return pl.pallas_call(
        comm_kernel,
        name='adam_comm',
        out_shape=(
            jax.ShapeDtypeStruct((2, ROUNDS, BLOCKS) + TILE, bf16), flat, flat, flat,
            jax.ShapeDtypeStruct((BROWS, LANES), bf16),
        ),
        in_specs=[any_spec] * 4 + [vmem_spec] + [any_spec] * 3 + [vmem_spec],
        out_specs=(any_spec,) * 4 + (vmem_spec,),
        scratch_shapes=[
            pltpu.VMEM((NACC, BLOCKS) + TILE, f32),
            pltpu.VMEM((2, BLOCKS) + TILE, f32),
            pltpu.VMEM((ROUNDS, BLOCKS // 2) + TILE, f32),
            pltpu.VMEM((ROUNDS, BLOCKS // 4) + TILE, f32),
            pltpu.VMEM((ROUNDS, TILES) + TILE, f32),
            pltpu.VMEM((2 * 3 * RAW_ROWS * LANES,), f32),
            pltpu.VMEM((3, RAW_ROWS, LANES), f32),
            pltpu.VMEM((3, ROWS + 8, LANES), f32),
            pltpu.VMEM((2 * 3 * ROWS * LANES,), f32),
            pltpu.VMEM((3, BROWS, LANES), f32),
            pltpu.VMEM((ROUNDS, TILES) + TILE, bf16),
            pltpu.VMEM((3, BROWS, LANES), f32),
            pltpu.VMEM((4, BROWS, LANES), f32),
            pltpu.VMEM((3, BROWS, LANES), f32),
            pltpu.VMEM((4, BROWS, LANES), bf16),
            pltpu.VMEM((4, BROWS, LANES), bf16),
            dma((NACC, 2)), dma((2,)), dma((2, 2)),
            dma((ROUNDS, 3)), dma((ROUNDS, 3, 3)),
            dma((ROUNDS, 3)), dma((ROUNDS, 3, 3)),
            dma((ROUNDS, 4)), dma((ROUNDS, 4)),
            dma((ROUNDS,)), dma((2,)), dma((2,)),
            dma((8,)), dma((8,)), dma((2,)), dma((2,)),
            pltpu.SemaphoreType.REGULAR,
        ],
        compiler_params=pltpu.CompilerParams(collective_id=0, has_side_effects=True, vmem_limit_bytes=67043328),
    )(*grads, gb, *olds, mvwb)


RING = 48
AHEAD = 28
CHIP_BLOCK = ROWS * LANES
CHIP_COUNT = 1968576
PARTS = 20
PER_PART = TENSOR_GROUPS[-1] // PARTS


def chip_group(pair, i):
    j = i - 2
    wide = 16 + 48 * (j // 6) + 24 * ((j % 6) // 3) + 3 * pair + j % 3
    first = jnp.where(i < 2, 1, 0)
    return first * (2 * pair + i) + (1 - first) * wide


def put_rows(rows, chip, first, count):
    def body(k):
        row = pl.multiple_of(first + k * 8, 8)
        flat = rows[pl.ds(row, 8), :].reshape(1, TILE_SIZE).astype(jnp.bfloat16)
        chip[:, pl.ds(pl.multiple_of(row * LANES, TILE_SIZE), TILE_SIZE)] = flat

    loop(count // 8, body, unroll=True)


def flatten_group(i, tiles, rows, chip, quarter):
    wide = (i >= 2) & (i < 14)

    def relay(stride):
        for u in range(4):
            row = quarter * 192 + u * (48 if stride == 6 else 6)
            for j in range(6):
                rows[pl.ds(row + j, 8, stride=stride), :] = tiles[quarter * 24 + u * 6 + j].astype(jnp.float32)

    @pl.when(wide)
    def _():
        relay(24)

    @pl.when(jnp.logical_not(wide))
    def _():
        relay(6)

    put_rows(rows, chip, quarter * 192, 192)


def unpack_kernel(wst, tail, we, wa, wf, wh, chip, buf, tiles, rows, where, in_sem, out_sem, sem):
    me = device_number()
    bits = chip_bits(me)
    pair = me // 2
    outs = (we, wa, wf, wh)
    total = TENSOR_GROUPS[-1]
    i = pl.program_id(0)

    def fill(d):
        diff = [(p + q) % 2 for p, q in zip(bits, chip_bits(d))]
        rels = [sum((1 << j) * diff[(k + j) % 3] for j in range(3)) for k in range(3)]
        for r in range(ROUNDS):
            for t, n, first, base in SLOTS:
                at = ((d % 2) * ROUNDS + r) * BLOCKS + base + rels[(t + r) % 3] * n
                where[(d * ROUNDS + r) * 3 + t] = at

    def fetch(group, dst, sem):
        for t, n, first, base in SLOTS:
            src = wst.at[pl.ds(where[group * 3 + t], n)]
            pltpu.make_async_copy(src, dst.at[pl.ds(first, n)], sem).start()

    def fetch_wait(dst, sem):
        pltpu.make_async_copy(wst.at[top(TILES)], dst, sem).wait()

    def start_in(g):
        slot = lax.rem(g, RING)
        fetch(g, buf.at[slot], in_sem.at[slot])

    def wait_out(g):
        slot = lax.rem(g, RING)
        pltpu.make_async_copy(buf.at[slot], wa.at[top(TILES)], out_sem.at[slot]).wait()

    def move(g):
        nxt = g + AHEAD

        @pl.when(nxt < total)
        def _():
            @pl.when(nxt >= RING)
            def _():
                wait_out(nxt)

            start_in(nxt)

        slot = lax.rem(g, RING)
        fetch_wait(buf.at[slot], in_sem.at[slot])
        for ref, lo, hi in zip(outs, TENSOR_GROUPS, TENSOR_GROUPS[1:]):
            @pl.when((g >= lo) & (g < hi))
            def _(ref=ref, lo=lo):
                pltpu.make_async_copy(buf.at[slot], ref.at[pl.ds((g - lo) * TILES, TILES)], out_sem.at[slot]).start()

    def start_part(k):
        fetch(chip_group(pair, k), tiles.at[k % 2], sem.at[k % 2])

    @pl.when(i == 0)
    def _():
        loop(2 * 8, fill)
        loop(AHEAD, start_in)
        start_part(0)

    @pl.when(i + 1 < PARTS)
    def _():
        start_part(i + 1)

    @pl.when(i < PARTS)
    def _():
        slot = i % 2
        fetch_wait(tiles.at[slot], sem.at[slot])

        def body(quarter):
            for k in range(2):
                move(i * PER_PART + quarter * 2 + k)
            flatten_group(i, tiles.at[slot], rows, chip, quarter)

        loop(PER_PART // 2, body)

    @pl.when(i == PARTS)
    def _():
        put_rows(tail, chip, 0, 24)
        loop(RING, wait_out)


def unpack_call(wst, tail):
    any_spec = pl.BlockSpec(memory_space=pl.ANY)
    sizes = [hi - lo for lo, hi in zip(TENSOR_GROUPS, TENSOR_GROUPS[1:])]
    bf16 = jnp.bfloat16
    dma = pltpu.SemaphoreType.DMA
    return pl.pallas_call(
        unpack_kernel,
        name='unpack',
        grid=(PARTS + 1,),
        out_shape=tuple(jax.ShapeDtypeStruct((n * TILES,) + TILE, bf16) for n in sizes)
        + (jax.ShapeDtypeStruct((1, CHIP_COUNT), bf16),),
        in_specs=[any_spec, pl.BlockSpec((24, LANES), lambda i: (0, 0))],
        out_specs=(any_spec,) * 4 + (pl.BlockSpec((1, CHIP_BLOCK), lambda i: (0, i)),),
        scratch_shapes=[
            pltpu.VMEM((RING, TILES) + TILE, bf16),
            pltpu.VMEM((2, TILES) + TILE, bf16),
            pltpu.VMEM((ROWS, LANES), jnp.float32),
            pltpu.SMEM((3 * TENSOR_GROUPS[-1],), jnp.int32),
            dma((RING,)), dma((RING,)), dma((2,)),
        ],
    )(wst, tail)


def to_tiles(x):
    width = x.shape[-1] // LANES
    return x.reshape(-1, 8, width, LANES).transpose(0, 2, 1, 3).reshape(-1, 8, LANES)


def from_tiles(x, shape):
    width = shape[-1] // LANES
    return x.reshape(-1, width, 8, LANES).transpose(0, 2, 1, 3).reshape(shape)


def solution(mesh):
    def local_step(g_embed, g_attn, g_ffn_in, g_ffn_out, g_vec, m_shard, v_shard, w_shard):
        d = device_number()
        mats = (g_embed, g_attn, g_ffn_in, g_ffn_out)
        shapes = [g.shape[1:] for g in mats]
        grads = [to_tiles(g) for g in mats]
        gb = jnp.pad(g_vec.reshape(-1, LANES), ((BPAD, 0), (0, 0)))
        shards = (m_shard, v_shard, w_shard)
        ends = jnp.stack([x[SHARD - BTAIL:].reshape(-1, LANES) for x in shards])
        mvwb = jnp.pad(ends, ((0, 0), (BPAD, 0), (0, 0)))
        wst, *new, wb = comm_call(grads, gb, shards, mvwb)
        new = [lax.slice(x, (BROWS * LANES,), (BROWS * LANES + SHARD,)) for x in new]
        wb_vec = wb[BPAD:].reshape(g_vec.shape[1:])
        part = g_vec.shape[2] // 8
        tail = lax.dynamic_slice(wb_vec, (0, (d // 2) * part), (2, part)).reshape(-1).astype(jnp.float32)
        tail = jnp.pad(tail, (0, 24 * LANES - 2 * part)).reshape(24, LANES)
        *packed, chip = unpack_call(wst.reshape((-1,) + TILE), tail)
        tensors = [from_tiles(x, shape) for x, shape in zip(packed, shapes)]
        return tuple(new) + tuple(tensors) + (wb_vec, chip)

    return jax.shard_map(local_step, mesh=mesh, in_specs=(P(MESH_AXES),) * 8,
                         out_specs=(P(MESH_AXES),) * 3 + (P(),) * 5 + (P(MESH_AXES),), check_vma=False)
```

time: 1150 us -> 369 us (0.32)
  waiting for transfers between devices: 860 us -> 0 us
  Pallas kernels: 0 us -> 351 us
  local copies, waits for them, and re-layouts: 262 us -> 14.9 us
  between operations: 14.2 us -> 0.72 us
    unnamed x4 -> x0, waiting for transfers between devices: 860 us -> none
    pallas_call x0 -> x2, Pallas kernels: none -> 351 us  [the longest x1 321 us: comm_call(): pl.pallas_call(comm_kernel, name='adam_comm', out_shape=(jax.ShapeDtypeSt...]
    unnamed x40 -> x6, local copies, waits for them, and re-layouts: 116 us -> 0.01 us
    reshape x10 -> x2, local copies, waits for them, and re-layouts: 76.1 us -> 1 us  [the longest x1 0.95 us: local_step(): gb = jnp.pad(g_vec.reshape(-1, LANES), ((BPAD, 0), (0, 0)))]
    broadcast_in_dim x1 -> x0, local copies, waits for them, and re-layouts: 38.9 us -> none  [own_chip_block(): return jnp.concatenate(block_list)[None, :]]
    slice x6 -> x4, local copies, waits for them, and re-layouts: 25.7 us -> 11.1 us  [the longest x3 11.1 us: local_step(): lax.slice(x, (BROWS * LANES,), (BROWS * LANES + SHARD,))]
  transfers between devices with their start and end apart: 2 -> 0, of which waited for: 2 -> 0; matrix products, arithmetic and copies ran while one was open for 0% -> 0% of each run, Pallas kernels for 0% -> 0%
where the time goes in v1:
time: 369 us; the launch traced here: 368 us
  Pallas kernels  351 us (95%)
  local copies, waits for them, and re-layouts  14.9 us (4%)
    pallas_call x1, Pallas kernels, comm_call(): pl.pallas_call(comm_kernel, name='adam_comm', out_shape=(jax.ShapeDtypeSt...  321 us
    pallas_call x1, Pallas kernels, unpack_call(): pl.pallas_call(unpack_kernel, name='unpack', grid=(PARTS + 1,), out_shape...  30.6 us
    slice x3, local copies, waits for them, and re-layouts, local_step(): lax.slice(x, (BROWS * LANES,), (BROWS * LANES + SHARD,))  11.1 us

profile of v1, /device:TPU:0, one launch (start us, length us, event | category | flops | bytes accessed | tf_op | source)
XLA Modules:
  0.0 368.2 jit_solution(5366710189020815733)
XLA Ops:
  0.7 1.0 reshape.91
  1.6 0.6 pad.13.gb
  2.3 1.0 slice_bitcast_fusion.2
  3.2 1.0 slice_bitcast_fusion
  4.3 0.7 select_maximum_fusion.mvwb
  5.0 320.6 %adam_comm.1 = (bf16[2,10,768,8,128]{4,3,2,1,0:T(8,128)(2,1)}, f32[1024000]{0:T(1024)}, f32[1024000]{0:T(1024)}, f32[1024000]{0:T(1024)}, bf16[160,128]{1,0:T(8,128)(2,1)}) custom-call(f32[1536,8,128]{2,1,0:T(8,128)} %bitcast.54, f32[4608,8,128]{2,1,0:T(8,128)} %bitcast.51, f32[4608,8,128]{2,1,0:T(8,128)} %bitcast.52, f32[4608,8,128]{2,1,0:T(8,128)} %bitcast.53, ...), custom_call_target="tpu_custom_call" | custom-call | tf_op jit(solution)/shard_map/adam_comm/pallas_call | solution.py:438
  325.6 0.0 copy-start.2
  325.6 4.3 %slice.24 = f32[984288]{0:T(1024)} slice(f32[1024000]{0:T(1024)} %get-tuple-element.19), slice={[20480:1004768]} | slice | bytes 7874304 | tf_op jit(solution)/shard_map/slice | solution.py:645
  329.9 0.0 copy-done.2
  330.0 0.0 copy-start.1
  330.0 0.1 constant_dynamic-slice_fusion
  330.1 0.1 convert_element_type.10
  330.1 0.0 copy-start
  330.1 0.6 bitcast_convert_fusion.tail
  330.8 4.6 %slice.25 = f32[984288]{0:T(1024)} slice(f32[1024000]{0:T(1024)} %get-tuple-element.20), slice={[20480:1004768]} | slice | bytes 7874304 | tf_op jit(solution)/shard_map/slice | solution.py:645
  335.3 0.0 copy-done
  335.4 2.2 slice.26
  337.5 0.0 copy-done.1
  337.5 30.6 %unpack.1 = (bf16[1536,8,128]{2,1,0:T(8,128)(2,1)}, bf16[4608,8,128]{2,1,0:T(8,128)(2,1)}, bf16[4608,8,128]{2,1,0:T(8,128)(2,1)}, bf16[4608,8,128]{2,1,0:T(8,128)(2,1)}, bf16[1,1968576]{1,0:T(2,128)(2,1)}) custom-call(bf16[15360,8,128]{2,1,0:T(8,128)(2,1)} %bitcast.50, f32[24,128]{1,0:T(8,128)} %bitcast_convert_fusion.tail), custom_call_target="tpu_custom_call" | custom-call | tf_op jit(solution)/shard_map/unpack/pallas_call | solution.py:606
  (2 shorter events, 0.1 us)
Async XLA Ops:
  325.6 4.3 %copy-start.2 = (bf16[160,128]{1,0:T(8,128)(2,1)S(1)}, bf16[160,128]{1,0:T(8,128)(2,1)}, u32[]{:S(2)}) copy-start(bf16[160,128]{1,0:T(8,128)(2,1)} %get-tuple-element.23) | copy-start | bytes 122884
  330.0 7.6 %copy-start.1 = (bf16[2,9984]{1,0:T(2,128)(2,1)}, bf16[2,9984]{1,0:T(2,128)(2,1)S(1)}, u32[]{:S(2)}) copy-start(bf16[2,9984]{1,0:T(2,128)(2,1)S(1)} %reshape.93) | copy-start | bytes 119812
  330.1 5.2 %copy-start = (f32[1024000]{0:T(1024)S(1)}, f32[1024000]{0:T(1024)}, u32[]{:S(2)}) copy-start(f32[1024000]{0:T(1024)} %get-tuple-element.21) | copy-start | bytes 12288004

commit v2 on v1

--- a/solution.py
+++ b/solution.py
@@ -17,7 +17,7 @@
 TILE_SIZE = 1024
 ROUNDS = 10
 TILES = 96
-SLOTS = ((0, 48, 0, 0), (1, 24, 48, 384), (2, 24, 72, 576))
+SLOTS = ((0, 36, 0, 0), (1, 30, 36, 288), (2, 30, 66, 528))
 BLOCKS = 8 * TILES
 TENSOR_GROUPS = (0, 16, 64, 112, 160)
 ROWS = 768
@@ -28,7 +28,9 @@
 BROWS = 160
 BPAD = BROWS - BTAIL // 128
 RAW_ROWS = ROWS + BROWS
-OUT_ROWS = ROUNDS * ROWS + 2 * BROWS
+PARTS = 20
+NEW_ROWS = ROUNDS * ROWS // PARTS
+OUT_ROWS = NEW_ROWS + ROUNDS * ROWS + BROWS
 NACC = 5
 STAGES = ROUNDS + 6
 MESH = pl.DeviceIdType.MESH
@@ -72,9 +74,9 @@
     return (d // 2) % 2, (d // 4) % 2, d // 8
 
 
-def comm_kernel(ge, ga, gf, gh, gb, m1, v1, w1, mvwb,
+def comm_kernel(ge, ga, gf, gh, gvec, m1, v1, w1, ends,
                 wst, m_out, v_out, w_out, wb_out,
-                acc, sib, l1, l2, l3, flat_in, raw, mv, flat_out, heads, wt, bs, bl, bout, wbs, wbl,
+                acc, sib, l1, l2, l3, flat_in, raw, mv, flat_out, heads, wt, mvwb, gb, bs, bl, bout, wbs, wbl,
                 own_sem, sib_send, sib_recv, rs_send, rs_recv, ag_send, ag_recv, fw_send, fw_recv,
                 loc_sem, in_sem, out_sem, b_send, b_recv, end_sem, head_sem, free_sem):
     me = device_number()
@@ -101,8 +103,11 @@
                                             device_id=mesh_id(dev), device_id_type=MESH)
 
     def turned(r):
-        steps = [pick(deltas, lax.rem(r + j, 3)) for j in range(3)]
+        steps = [pick(deltas, lax.rem(2 * r + j, 3)) for j in range(3)]
         return [[steps[(t + j) % 3] for j in range(3)] for t in range(3)]
+
+    def block(d, r, first, n):
+        return wst.at[pl.ds((d * ROUNDS + r) * TILES + first, n)]
 
     def any_tiles(n):
         return ga.at[top(n)]
@@ -138,10 +143,10 @@
 
     def add_range(dst, src, n):
         def body(i):
-            at = pl.ds(i * 8, 8)
+            at = pl.ds(i * 6, 6)
             dst[at] = dst[at] + src[at]
 
-        loop(n // 8, body)
+        loop(n // 6, body)
 
     def when_round(r):
         return pl.when((r >= 0) & (r < ROUNDS))
@@ -165,7 +170,7 @@
         loop((RAW_ROWS - skip) // 8, body)
 
     def out_copy(ref, b, i, r, n):
-        at = pl.multiple_of((r * ROWS + BROWS - 1 - shift_rows) * LANES, LANES)
+        at = pl.multiple_of((r * ROWS + NEW_ROWS - 1 - shift_rows) * LANES, LANES)
         return pltpu.make_async_copy(flat_out.at[pl.ds((b * 3 + i) * ROWS * LANES, n * LANES)], ref.at[pl.ds(at, n * LANES)],
                                      out_sem.at[b])
 
@@ -187,6 +192,17 @@
             out_copy(ref, b, i, 0, n).wait()
 
     load_round(0)
+
+    gb[...] = jnp.zeros_like(gb)
+    mvwb[...] = jnp.zeros_like(mvwb)
+    for i, ref in olds:
+        mvwb[i, pl.ds(BPAD, BROWS - BPAD), :] = ends[pl.ds(i * (BROWS - BPAD), BROWS - BPAD), :]
+    for i in range(2):
+        def spread(k, i=i):
+            row = BPAD + i * (BTAIL // LANES // 2) + k
+            gb[pl.ds(row, 1), :] = gvec[pl.ds(i, 1), pl.ds(pl.multiple_of(k * LANES, LANES), LANES)]
+
+        loop(BTAIL // LANES // 2, spread)
 
     @pl.when(me < 15)
     def _():
@@ -325,11 +341,11 @@
                 adam_pass(6)
 
             for t, n, first, base in SLOTS:
-                src = wt.at[r, pl.ds(first, n)]
-                remote(src, wst.at[core, r, pl.ds(base + n, n)], ag_send.at[r, 0], ag_recv.at[r, t, 0],
+                remote(wt.at[r, pl.ds(first, n)], block(me, r, first, n), ag_send.at[r, 0], ag_recv.at[r, t, 0],
                        me + steps[t][0]).start()
-                remote(src, wst.at[core, r, pl.ds(base, n)], fw_send.at[r, 0], fw_recv.at[r, 0], mate).start()
-                pltpu.make_async_copy(src, wst.at[core, r, pl.ds(base, n)], loc_sem.at[r]).start()
+            mine = block(me, r, 0, TILES)
+            remote(wt.at[r], mine, fw_send.at[r, 0], fw_recv.at[r, 0], mate).start()
+            pltpu.make_async_copy(wt.at[r], mine, loc_sem.at[r]).start()
 
             @pl.when((r == 0) & (me > 0))
             def _():
@@ -361,15 +377,20 @@
                 got = 1 << (j - 1)
                 steps = turned(r)
                 if j == 1:
-                    pltpu.make_async_copy(wt.at[r], wst.at[core, r, top(TILES)], loc_sem.at[r]).wait()
+                    pltpu.make_async_copy(wt.at[r], block(me, r, 0, TILES), loc_sem.at[r]).wait()
                 for t, n, first, base in SLOTS:
-                    here = wst.at[core, r, pl.ds(base + got * n, got * n)]
-                    remote(here, here, ag_send.at[r, j - 1], ag_recv.at[r, t, j - 1], mate).wait_recv()
+                    part = wst.at[top(got * n)]
+                    remote(part, part, ag_send.at[r, j - 1], ag_recv.at[r, t, j - 1], mate).wait_recv()
+                    held = [me]
+                    for step in steps[t][:j]:
+                        held = held + [d + step for d in held]
                     if j < 3:
-                        remote(wst.at[core, r, pl.ds(base, 2 * got * n)],
-                               wst.at[core, r, pl.ds(base + 2 * got * n, 2 * got * n)],
-                               ag_send.at[r, j], ag_recv.at[r, t, j], me + steps[t][j]).start()
-                    remote(here, here, fw_send.at[r, j], fw_recv.at[r, j], mate).start()
+                        for d in held:
+                            here = block(d, r, first, n)
+                            remote(here, here, ag_send.at[r, j], ag_recv.at[r, t, j], me + steps[t][j]).start()
+                    for d in held[got:]:
+                        here = block(d, r, first, n)
+                        remote(here, here, fw_send.at[r, j], fw_recv.at[r, j], mate).start()
 
         for j in range(9):
             @pl.when(s == j)
@@ -417,10 +438,10 @@
                 rs_wait(r, j)
 
         for j in range(3):
-            part = wst.at[0, 0, top(TILES << j)]
+            part = wst.at[top(TILES << j)]
             remote(part, part, ag_send.at[r, j], ag_recv.at[r, 0, j], mate).wait_send()
         for j in range(4):
-            part = wst.at[0, 0, top(TILES << max(j - 1, 0))]
+            part = wst.at[top(TILES << max(j - 1, 0))]
             remote(part, part, fw_send.at[r, j], fw_recv.at[r, j], mate).wait_send()
             remote(part, part, fw_send.at[r, j], fw_recv.at[r, j], mate).wait_recv()
 
@@ -429,7 +450,7 @@
     wait_out(0, BROWS)
 
 
-def comm_call(grads, gb, olds, mvwb):
+def comm_call(grads, gvec, olds, ends):
     any_spec = pl.BlockSpec(memory_space=pl.ANY)
     vmem_spec = pl.BlockSpec(memory_space=pltpu.VMEM)
     f32, bf16 = jnp.float32, jnp.bfloat16
@@ -439,7 +460,7 @@
         comm_kernel,
         name='adam_comm',
         out_shape=(
-            jax.ShapeDtypeStruct((2, ROUNDS, BLOCKS) + TILE, bf16), flat, flat, flat,
+            jax.ShapeDtypeStruct((TENSOR_GROUPS[-1] * TILES,) + TILE, bf16), flat, flat, flat,
             jax.ShapeDtypeStruct((BROWS, LANES), bf16),
         ),
         in_specs=[any_spec] * 4 + [vmem_spec] + [any_spec] * 3 + [vmem_spec],
@@ -457,6 +478,8 @@
             pltpu.VMEM((3, BROWS, LANES), f32),
             pltpu.VMEM((ROUNDS, TILES) + TILE, bf16),
             pltpu.VMEM((3, BROWS, LANES), f32),
+            pltpu.VMEM((BROWS, LANES), f32),
+            pltpu.VMEM((3, BROWS, LANES), f32),
             pltpu.VMEM((4, BROWS, LANES), f32),
             pltpu.VMEM((3, BROWS, LANES), f32),
             pltpu.VMEM((4, BROWS, LANES), bf16),
@@ -470,14 +493,15 @@
             pltpu.SemaphoreType.REGULAR,
         ],
         compiler_params=pltpu.CompilerParams(collective_id=0, has_side_effects=True, vmem_limit_bytes=67043328),
-    )(*grads, gb, *olds, mvwb)
-
-
-RING = 48
-AHEAD = 28
+    )(*grads, gvec, *olds, ends)
+
+
+RING = 16
+AHEAD = 8
+HALF = BLOCKS // 2
+MOVES = TENSOR_GROUPS[-1] * TILES // HALF
 CHIP_BLOCK = ROWS * LANES
 CHIP_COUNT = 1968576
-PARTS = 20
 PER_PART = TENSOR_GROUPS[-1] // PARTS
 
 
@@ -517,80 +541,66 @@
     put_rows(rows, chip, quarter * 192, 192)
 
 
-def unpack_kernel(wst, tail, we, wa, wf, wh, chip, buf, tiles, rows, where, in_sem, out_sem, sem):
+def unpack_kernel(wst, tail, m1, v1, w1, we, wa, wf, wh, chip, m2, v2, w2, buf, tiles, rows,
+                  in_sem, out_sem, sem):
     me = device_number()
-    bits = chip_bits(me)
     pair = me // 2
     outs = (we, wa, wf, wh)
-    total = TENSOR_GROUPS[-1]
     i = pl.program_id(0)
-
-    def fill(d):
-        diff = [(p + q) % 2 for p, q in zip(bits, chip_bits(d))]
-        rels = [sum((1 << j) * diff[(k + j) % 3] for j in range(3)) for k in range(3)]
-        for r in range(ROUNDS):
-            for t, n, first, base in SLOTS:
-                at = ((d % 2) * ROUNDS + r) * BLOCKS + base + rels[(t + r) % 3] * n
-                where[(d * ROUNDS + r) * 3 + t] = at
-
-    def fetch(group, dst, sem):
-        for t, n, first, base in SLOTS:
-            src = wst.at[pl.ds(where[group * 3 + t], n)]
-            pltpu.make_async_copy(src, dst.at[pl.ds(first, n)], sem).start()
-
-    def fetch_wait(dst, sem):
-        pltpu.make_async_copy(wst.at[top(TILES)], dst, sem).wait()
-
-    def start_in(g):
-        slot = lax.rem(g, RING)
-        fetch(g, buf.at[slot], in_sem.at[slot])
-
-    def wait_out(g):
-        slot = lax.rem(g, RING)
-        pltpu.make_async_copy(buf.at[slot], wa.at[top(TILES)], out_sem.at[slot]).wait()
-
-    def move(g):
-        nxt = g + AHEAD
-
-        @pl.when(nxt < total)
-        def _():
-            @pl.when(nxt >= RING)
-            def _():
-                wait_out(nxt)
-
-            start_in(nxt)
-
-        slot = lax.rem(g, RING)
-        fetch_wait(buf.at[slot], in_sem.at[slot])
-        for ref, lo, hi in zip(outs, TENSOR_GROUPS, TENSOR_GROUPS[1:]):
-            @pl.when((g >= lo) & (g < hi))
-            def _(ref=ref, lo=lo):
-                pltpu.make_async_copy(buf.at[slot], ref.at[pl.ds((g - lo) * TILES, TILES)], out_sem.at[slot]).start()
-
-    def start_part(k):
-        fetch(chip_group(pair, k), tiles.at[k % 2], sem.at[k % 2])
+    news = ((m1, m2), (v1, v2), (w1, w2))
+
+    def some(k):
+        return wst.at[pl.ds(k * HALF, HALF)]
+
+    def start_in(k):
+        slot = lax.rem(k, RING)
+        pltpu.make_async_copy(some(k), buf.at[slot], in_sem.at[slot]).start()
+
+    def wait_out(k):
+        slot = lax.rem(k, RING)
+        pltpu.make_async_copy(buf.at[slot], wa.at[top(HALF)], out_sem.at[slot]).wait()
+
+    def part_copy(k):
+        src = wst.at[pl.ds(chip_group(pair, k) * TILES, TILES)]
+        return pltpu.make_async_copy(src, tiles.at[k % 2], sem.at[k % 2])
+
+    for src, dst in news:
+        dst[...] = src[...]
 
     @pl.when(i == 0)
     def _():
-        loop(2 * 8, fill)
+        part_copy(0).start()
         loop(AHEAD, start_in)
-        start_part(0)
+
+    def move(k):
+        nxt = k + AHEAD
+
+        @pl.when((nxt >= RING) & (nxt < MOVES))
+        def _():
+            wait_out(nxt)
+
+        @pl.when(nxt < MOVES)
+        def _():
+            start_in(nxt)
+
+        slot = lax.rem(k, RING)
+        pltpu.make_async_copy(some(k), buf.at[slot], in_sem.at[slot]).wait()
+        for ref, lo, hi in zip(outs, TENSOR_GROUPS, TENSOR_GROUPS[1:]):
+            @pl.when((i * PER_PART >= lo) & (i * PER_PART < hi))
+            def _(ref=ref, lo=lo):
+                dst = ref.at[pl.ds(k * HALF - lo * TILES, HALF)]
+                pltpu.make_async_copy(buf.at[slot], dst, out_sem.at[slot]).start()
 
     @pl.when(i + 1 < PARTS)
     def _():
-        start_part(i + 1)
+        part_copy(i + 1).start()
 
     @pl.when(i < PARTS)
     def _():
-        slot = i % 2
-        fetch_wait(tiles.at[slot], sem.at[slot])
-
-        def body(quarter):
-            for k in range(2):
-                move(i * PER_PART + quarter * 2 + k)
-            flatten_group(i, tiles.at[slot], rows, chip, quarter)
-
-        loop(PER_PART // 2, body)
+        part_copy(i).wait()
+        for k in range(2):
+            move(2 * i + k)
+            loop(2, lambda q: flatten_group(i, tiles.at[i % 2], rows, chip, 2 * k + q))
 
     @pl.when(i == PARTS)
     def _():
@@ -598,7 +608,7 @@
         loop(RING, wait_out)
 
 
-def unpack_call(wst, tail):
+def unpack_call(wst, tail, new):
     any_spec = pl.BlockSpec(memory_space=pl.ANY)
     sizes = [hi - lo for lo, hi in zip(TENSOR_GROUPS, TENSOR_GROUPS[1:])]
     bf16 = jnp.bfloat16
@@ -608,17 +618,17 @@
         name='unpack',
         grid=(PARTS + 1,),
         out_shape=tuple(jax.ShapeDtypeStruct((n * TILES,) + TILE, bf16) for n in sizes)
-        + (jax.ShapeDtypeStruct((1, CHIP_COUNT), bf16),),
-        in_specs=[any_spec, pl.BlockSpec((24, LANES), lambda i: (0, 0))],
-        out_specs=(any_spec,) * 4 + (pl.BlockSpec((1, CHIP_BLOCK), lambda i: (0, i)),),
+        + (jax.ShapeDtypeStruct((1, CHIP_COUNT), bf16),) + (jax.ShapeDtypeStruct((SHARD,), jnp.float32),) * 3,
+        in_specs=[any_spec, pl.BlockSpec((24, LANES), lambda i: (0, 0))] + [pl.BlockSpec((NEW_ROWS * LANES,), lambda i: (i + 1,))] * 3,
+        out_specs=(any_spec,) * 4 + (pl.BlockSpec((1, CHIP_BLOCK), lambda i: (0, i)),)
+        + (pl.BlockSpec((NEW_ROWS * LANES,), lambda i: (i,)),) * 3,
         scratch_shapes=[
-            pltpu.VMEM((RING, TILES) + TILE, bf16),
+            pltpu.VMEM((RING, HALF) + TILE, bf16),
             pltpu.VMEM((2, TILES) + TILE, bf16),
             pltpu.VMEM((ROWS, LANES), jnp.float32),
-            pltpu.SMEM((3 * TENSOR_GROUPS[-1],), jnp.int32),
             dma((RING,)), dma((RING,)), dma((2,)),
         ],
-    )(wst, tail)
+    )(wst, tail, *new)
 
 
 def to_tiles(x):
@@ -637,19 +647,16 @@
         mats = (g_embed, g_attn, g_ffn_in, g_ffn_out)
         shapes = [g.shape[1:] for g in mats]
         grads = [to_tiles(g) for g in mats]
-        gb = jnp.pad(g_vec.reshape(-1, LANES), ((BPAD, 0), (0, 0)))
         shards = (m_shard, v_shard, w_shard)
-        ends = jnp.stack([x[SHARD - BTAIL:].reshape(-1, LANES) for x in shards])
-        mvwb = jnp.pad(ends, ((0, 0), (BPAD, 0), (0, 0)))
-        wst, *new, wb = comm_call(grads, gb, shards, mvwb)
-        new = [lax.slice(x, (BROWS * LANES,), (BROWS * LANES + SHARD,)) for x in new]
+        ends = jnp.concatenate([x[SHARD - BTAIL:] for x in shards]).reshape(-1, LANES)
+        wst, *new, wb = comm_call(grads, g_vec[0], shards, ends)
         wb_vec = wb[BPAD:].reshape(g_vec.shape[1:])
         part = g_vec.shape[2] // 8
         tail = lax.dynamic_slice(wb_vec, (0, (d // 2) * part), (2, part)).reshape(-1).astype(jnp.float32)
         tail = jnp.pad(tail, (0, 24 * LANES - 2 * part)).reshape(24, LANES)
-        *packed, chip = unpack_call(wst.reshape((-1,) + TILE), tail)
+        *packed, chip, m_new, v_new, w_new = unpack_call(wst, tail, new)
         tensors = [from_tiles(x, shape) for x, shape in zip(packed, shapes)]
-        return tuple(new) + tuple(tensors) + (wb_vec, chip)
+        return (m_new, v_new, w_new) + tuple(tensors) + (wb_vec, chip)
 
     return jax.shard_map(local_step, mesh=mesh, in_specs=(P(MESH_AXES),) * 8,
                          out_specs=(P(MESH_AXES),) * 3 + (P(),) * 5 + (P(MESH_AXES),), check_vma=False)

time: 369 us -> 359 us (0.973)
  local copies, waits for them, and re-layouts: 14.9 us -> 3.03 us
    slice x3 -> x0, local copies, waits for them, and re-layouts: 11.1 us -> none  [local_step(): lax.slice(x, (BROWS * LANES,), (BROWS * LANES + SHARD,))]
    pallas_call x1, Pallas kernels: 30.6 us -> 36.2 us  [unpack_call(): pl.pallas_call(unpack_kernel, name='unpack', grid=(PARTS + 1,), out_shape...]
where the time goes in v2:
time: 359 us; the launch traced here: 358 us
  Pallas kernels  353 us (98%)
    pallas_call x1, Pallas kernels, comm_call(): pl.pallas_call(comm_kernel, name='adam_comm', out_shape=(jax.ShapeDtypeSt...  317 us
    pallas_call x1, Pallas kernels, unpack_call(): pl.pallas_call(unpack_kernel, name='unpack', grid=(PARTS + 1,), out_shape...  36.2 us

profile of v2, /device:TPU:0, one launch (start us, length us, event | category | flops | bytes accessed | tf_op | source)
XLA Modules:
  0.0 358.1 jit_solution(10839177244604234190)
XLA Ops:
  0.7 1.0 slice_bitcast_fusion.2
  1.6 1.0 slice_bitcast_fusion
  2.7 0.7 pad_maximum_fusion.ends
  3.4 316.9 %adam_comm.1 = (bf16[15360,8,128]{2,1,0:T(8,128)(2,1)}, f32[1052672]{0:T(1024)}, f32[1052672]{0:T(1024)}, f32[1052672]{0:T(1024)}, bf16[160,128]{1,0:T(8,128)(2,1)}) custom-call(f32[1536,8,128]{2,1,0:T(8,128)} %bitcast.53, f32[4608,8,128]{2,1,0:T(8,128)} %bitcast.50, f32[4608,8,128]{2,1,0:T(8,128)} %bitcast.51, f32[4608,8,128]{2,1,0:T(8,128)} %bitcast.52, ...), custom_call_target="tpu_custom_call" | custom-call | tf_op jit(solution)/shard_map/adam_comm/pallas_call | solution.py:459
  320.3 0.8 slice.15
  321.2 0.0 copy-start
  321.2 0.1 constant_dynamic-slice_fusion
  321.3 0.1 convert_element_type.6
  321.3 0.6 bitcast_convert_fusion.tail
  322.0 36.2 %unpack.1 = (bf16[1536,8,128]{2,1,0:T(8,128)(2,1)}, bf16[4608,8,128]{2,1,0:T(8,128)(2,1)}, bf16[4608,8,128]{2,1,0:T(8,128)(2,1)}, bf16[4608,8,128]{2,1,0:T(8,128...) custom-call(bf16[15360,8,128]{2,1,0:T(8,128)(2,1)} %get-tuple-element.22.wst, ...), custom_call_target="tpu_custom_call" | custom-call | tf_op jit(solution)/shard_map/unpack/pallas_call | solution.py:616
  358.1 0.0 copy-done
  (1 shorter events, 0.0 us)
Async XLA Ops:
  321.2 37.0 %copy-start = (bf16[2,9984]{1,0:T(2,128)(2,1)}, bf16[2,9984]{1,0:T(2,128)(2,1)S(1)}, u32[]{:S(2)}) copy-start(bf16[2,9984]{1,0:T(2,128)(2,1)S(1)} %reshape.89) | copy-start | bytes 119812

commit v3 on v2

--- a/solution.py
+++ b/solution.py
@@ -102,6 +102,19 @@
         return pltpu.make_async_remote_copy(src_ref=src, dst_ref=dst, send_sem=ssem, recv_sem=rsem,
                                             device_id=mesh_id(dev), device_id_type=MESH)
 
+    def sized(number, use):
+        for c in range(4):
+            @pl.when((number + 3) // 4 == c + 1)
+            def _(c=c):
+                use((c + 1) * BROWS // 4)
+
+    def ends_copy(n, dev):
+        at = pl.ds(BROWS - n, n)
+        return remote(mvwb.at[:, at], raw.at[:, at], end_sem.at[0], end_sem.at[1], dev)
+
+    def heads_copy(n, dev):
+        return remote(mv.at[:, pl.ds(8, n)], heads.at[:, top(n)], head_sem.at[0], head_sem.at[1], dev)
+
     def turned(r):
         steps = [pick(deltas, lax.rem(2 * r + j, 3)) for j in range(3)]
         return [[steps[(t + j) % 3] for j in range(3)] for t in range(3)]
@@ -135,9 +148,9 @@
                         def _(ref=ref, lo=lo, other=other, group=group):
                             src = ref.at[pl.ds((group - lo) * TILES + first, n)]
                             if other:
-                                remote(src, sib.at[b, at], sib_send.at[b], sib_recv.at[b, rel // 4], mate).start()
+                                remote(src, sib.at[b, at], sib_send.at[b], sib_recv.at[b, rel], mate).start()
                             else:
-                                pltpu.make_async_copy(src, acc.at[a, at], own_sem.at[a, rel // 4]).start()
+                                pltpu.make_async_copy(src, acc.at[a, at], own_sem.at[a, rel]).start()
 
         loop(8, body)
 
@@ -193,22 +206,41 @@
 
     load_round(0)
 
-    gb[...] = jnp.zeros_like(gb)
     mvwb[...] = jnp.zeros_like(mvwb)
     for i, ref in olds:
         mvwb[i, pl.ds(BPAD, BROWS - BPAD), :] = ends[pl.ds(i * (BROWS - BPAD), BROWS - BPAD), :]
-    for i in range(2):
-        def spread(k, i=i):
-            row = BPAD + i * (BTAIL // LANES // 2) + k
-            gb[pl.ds(row, 1), :] = gvec[pl.ds(i, 1), pl.ds(pl.multiple_of(k * LANES, LANES), LANES)]
-
-        loop(BTAIL // LANES // 2, spread)
-
     @pl.when(me < 15)
     def _():
-        remote(mvwb, raw.at[:, top(BROWS)], end_sem.at[0], end_sem.at[1], me + 1).start()
+        sized(me + 1, lambda n: ends_copy(n, me + 1).start())
 
     def stage(s):
+        @when_round(s)
+        def _():
+            r, a, b = s, s % NACC, s % 2
+            steps = turned(r)
+
+            def sum_cores(rel):
+                src, some = any_tiles(TILES), top(TILES)
+                pltpu.make_async_copy(src, acc.at[a, some], own_sem.at[a, rel]).wait()
+                remote(src, sib.at[b, some], sib_send.at[b], sib_recv.at[b, rel], mate).wait_recv()
+                for t, n, first, base in SLOTS:
+                    at = pl.ds(base + rel * n, n)
+                    add_range(acc.at[a, at], sib.at[b, at], n)
+
+            def send_half(rel):
+                for t, n, first, base in SLOTS:
+                    remote(acc.at[a, pl.ds(base + rel * n, n)], l1.at[r, pl.ds(base // 2 + (rel - 4) * n, n)],
+                           rs_send.at[r, 0], rs_recv.at[r, t, 0], me + steps[t][0]).start()
+
+            for rel in reversed(range(8)):
+                sum_cores(rel)
+                if 3 <= rel < 7:
+                    send_half(rel + 1)
+
+            @pl.when(r + 2 < ROUNDS)
+            def _():
+                pl.semaphore_signal(free_sem, inc=1, device_id=mesh_id(mate), device_id_type=MESH)
+
         nxt = s + 1
 
         @pl.when((nxt >= NACC) & (nxt < ROUNDS))
@@ -227,6 +259,16 @@
 
         @pl.when(s == 2)
         def _():
+            gb[...] = jnp.zeros_like(gb)
+            for i in range(2):
+                def spread(k, i=i):
+                    row = BPAD + i * (BTAIL // LANES // 2) + k
+                    gb[pl.ds(row, 1), :] = gvec[pl.ds(i, 1), pl.ds(pl.multiple_of(k * LANES, LANES), LANES)]
+
+                loop(BTAIL // LANES // 2, spread)
+
+        @pl.when(s == 2)
+        def _():
             for i, ref in olds:
                 old_copy(ref, 0, i, BROWS).start()
 
@@ -234,32 +276,6 @@
         def _():
             for i, ref in olds:
                 old_copy(ref, s - 2, i, 0).start()
-
-        @when_round(s)
-        def _():
-            r, a, b = s, s % NACC, s % 2
-            steps = turned(r)
-
-            def loaded(part):
-                src, half = any_tiles(BLOCKS // 2), top(BLOCKS // 2)
-                pltpu.make_async_copy(src, acc.at[a, half], own_sem.at[a, part]).wait()
-                remote(src, sib.at[b, half], sib_send.at[b], sib_recv.at[b, part], mate).wait_recv()
-
-            loaded(1)
-            for t, n, first, base in SLOTS:
-                hi = pl.ds(base + 4 * n, 4 * n)
-                add_range(acc.at[a, hi], sib.at[b, hi], 4 * n)
-            for t, n, first, base in SLOTS:
-                remote(acc.at[a, pl.ds(base + 4 * n, 4 * n)], l1.at[r, pl.ds(base // 2, 4 * n)],
-                       rs_send.at[r, 0], rs_recv.at[r, t, 0], me + steps[t][0]).start()
-            loaded(0)
-            for t, n, first, base in SLOTS:
-                lo = pl.ds(base, 4 * n)
-                add_range(acc.at[a, lo], sib.at[b, lo], 4 * n)
-
-            @pl.when(r + 2 < ROUNDS)
-            def _():
-                pl.semaphore_signal(free_sem, inc=1, device_id=mesh_id(mate), device_id_type=MESH)
 
         for j, land, out in ((1, l1, l2), (2, l2, l3)):
             @when_round(s - j)
@@ -290,7 +306,7 @@
 
             @pl.when((r == 0) & (me > 0))
             def _():
-                remote(mvwb, raw.at[:, top(BROWS)], end_sem.at[0], end_sem.at[1], mate).wait_recv()
+                sized(me, lambda n: ends_copy(n, mate).wait_recv())
 
             @pl.when(r > 0)
             def _():
@@ -298,7 +314,7 @@
 
             @pl.when((r == 1) & (me > 0))
             def _():
-                remote(mv.at[:, pl.ds(8, BROWS)], heads, head_sem.at[0], head_sem.at[1], mate).wait_send()
+                sized(me, lambda n: heads_copy(n, mate).wait_send())
 
             for i, ref in outs:
                 mv[i, pl.ds(7, 1), :] = mv[i, pl.ds(ROWS + 7, 1), :]
@@ -349,7 +365,7 @@
 
             @pl.when((r == 0) & (me > 0))
             def _():
-                remote(mv.at[:, pl.ds(8, BROWS)], heads, head_sem.at[0], head_sem.at[1], me - 1).start()
+                sized(me, lambda n: heads_copy(n, me - 1).start())
 
             @pl.when(r >= 2)
             def _():
@@ -359,8 +375,8 @@
 
         @pl.when((s == ROUNDS + 3) & (me < 15))
         def _():
-            remote(mvwb, raw.at[:, top(BROWS)], end_sem.at[0], end_sem.at[1], mate).wait_send()
-            remote(mv.at[:, pl.ds(8, BROWS)], heads, head_sem.at[0], head_sem.at[1], mate).wait_recv()
+            sized(me + 1, lambda n: ends_copy(n, mate).wait_send())
+            sized(me + 1, lambda n: heads_copy(n, mate).wait_recv())
 
         @pl.when(s == ROUNDS + 3)
         def _():
@@ -393,7 +409,7 @@
                         remote(here, here, fw_send.at[r, j], fw_recv.at[r, j], mate).start()
 
         for j in range(9):
-            @pl.when(s == j)
+            @pl.when(s == j + 3)
             def _(j=j):
                 if j > 0:
                     i = j - 1
@@ -484,7 +500,7 @@
             pltpu.VMEM((3, BROWS, LANES), f32),
             pltpu.VMEM((4, BROWS, LANES), bf16),
             pltpu.VMEM((4, BROWS, LANES), bf16),
-            dma((NACC, 2)), dma((2,)), dma((2, 2)),
+            dma((NACC, 8)), dma((2,)), dma((2, 8)),
             dma((ROUNDS, 3)), dma((ROUNDS, 3, 3)),
             dma((ROUNDS, 3)), dma((ROUNDS, 3, 3)),
             dma((ROUNDS, 4)), dma((ROUNDS, 4)),

time: 359 us -> 356 us (level)
  no operation moved by 1% of the time
where the time goes in v3:
time: 356 us
  Pallas kernels  351 us (99%)
    pallas_call x1, Pallas kernels, comm_call(): pl.pallas_call(comm_kernel, name='adam_comm', out_shape=(jax.ShapeDtypeSt...  314 us
    pallas_call x1, Pallas kernels, unpack_call(): pl.pallas_call(unpack_kernel, name='unpack', grid=(PARTS + 1,), out_shape...  36.2 us

profile of v3, /device:TPU:0, one launch (start us, length us, event | category | flops | bytes accessed | tf_op | source)
XLA Modules:
  0.0 355.6 jit_solution(8941945933655214874)
XLA Ops:
  0.7 1.0 slice_bitcast_fusion.2
  1.6 1.0 slice_bitcast_fusion
  2.7 0.7 pad_maximum_fusion.ends
  3.4 314.4 %adam_comm.1 = (bf16[15360,8,128]{2,1,0:T(8,128)(2,1)}, f32[1052672]{0:T(1024)}, f32[1052672]{0:T(1024)}, f32[1052672]{0:T(1024)}, bf16[160,128]{1,0:T(8,128)(2,1)}) custom-call(f32[1536,8,128]{2,1,0:T(8,128)} %bitcast.53, f32[4608,8,128]{2,1,0:T(8,128)} %bitcast.50, f32[4608,8,128]{2,1,0:T(8,128)} %bitcast.51, f32[4608,8,128]{2,1,0:T(8,128)} %bitcast.52, ...), custom_call_target="tpu_custom_call" | custom-call | tf_op jit(solution)/shard_map/adam_comm/pallas_call | solution.py:475
  317.8 0.8 slice.15
  318.6 0.0 copy-start
  318.6 0.1 constant_dynamic-slice_fusion
  318.7 0.1 convert_element_type.6
  318.8 0.6 bitcast_convert_fusion.tail
  319.4 36.2 %unpack.1 = (bf16[1536,8,128]{2,1,0:T(8,128)(2,1)}, bf16[4608,8,128]{2,1,0:T(8,128)(2,1)}, bf16[4608,8,128]{2,1,0:T(8,128)(2,1)}, bf16[4608,8,128]{2,1,0:T(8,128...) custom-call(bf16[15360,8,128]{2,1,0:T(8,128)(2,1)} %get-tuple-element.22.wst, ...), custom_call_target="tpu_custom_call" | custom-call | tf_op jit(solution)/shard_map/unpack/pallas_call | solution.py:632
  355.6 0.0 copy-done
  (1 shorter events, 0.0 us)
Async XLA Ops:
  318.6 37.0 %copy-start = (bf16[2,9984]{1,0:T(2,128)(2,1)}, bf16[2,9984]{1,0:T(2,128)(2,1)S(1)}, u32[]{:S(2)}) copy-start(bf16[2,9984]{1,0:T(2,128)(2,1)S(1)} %reshape.89) | copy-start | bytes 119812
